TPU v7x, 32 devices: a whole 2x2x4 slice. The times are simulated.
32 devices in a mesh: groups: 2 (over x), sph: 16 (over z, y, core).
Axes of the slice: x: 2, y: 2, z: 4, core: 2. Of those that a mesh axis runs over, the one named last changes fastest.
Arguments:
- positions: float32 [512, 3], P('sph'), may hold values from -8 to 8
- wave_vectors: float32 [256, 3], replicated, may hold values from -5 to 5
- pattern: float32 [2, 448, 256], replicated, may hold values from -6 to 6
- dir_index: int32 [64], P('groups'), parts along dimension 0, may hold values from 0 to 255
- mie: float32 [2, 448, 512], P(None, None, 'sph'), may hold values from -0.9 to 0.9
- trans_table: bfloat16 [8, 2, 448, 448], replicated, may hold values from -0.1875 to 0.1875
- pair_route: int32 [1024, 1], P('sph'), may hold values from 0 to 15; in each aligned block of 64 rows (0 to 63, 64 to 127, ...) at most 8 rows name the same one
- pair_source: int32 [1024], P('sph'), may hold values from 0 to 15
- pair_target: int32 [1024], P('sph'), may hold values from 0 to 15
- pair_class: int32 [1024], P('sph'), may hold values from 0 to 7
Outputs:
- scattered: bfloat16 [896, 32768], P(None, ('groups', 'sph')), parts along dimension 1
- extinction: float32 [64], P('groups'), parts along dimension 0
There are 2 independent parts, one for each index of `groups`. A program takes and returns all parts, laid end to end along the dimension named above; an argument that names none is the same for every part. Nothing has to cross between parts.
Inputs may be any that keep to these rules, and one draw needn't show every extreme that they name: `pair_route`: among the rows of one device no device is named by more than 8 pairs, and in every draw some device is named by exactly 8 of them.
All inputs are finite; a program needn't handle non-finite values.
Results may differ from a plain program's by a relative error of at most 0.0051.
Values may be sent and summed in bfloat16 or wider, within the bound.
No kernel may reach another device: no remote copies, remote signals or barrier semaphores. Data moves between devices by JAX's collectives and lax.ppermute only.
A program may use at most 192 MiB of HBM per device.

v0:
```python
import jax
import jax.numpy as jnp
from jax import lax
from jax.sharding import PartitionSpec as P

BLOCK = 2
HIGHEST_PRECISION = lax.Precision.HIGHEST


def incident_field(positions, wave_vectors, pattern, dir_index):
    table_rows = wave_vectors.shape[0]
    select = (jnp.arange(table_rows, dtype=jnp.int32)[:, None] == dir_index[None, :]).astype(
        jnp.float32
    )
    directions = jnp.dot(select.T, wave_vectors, precision=HIGHEST_PRECISION)
    phases = (
        positions[:, 0:1] * directions[None, :, 0]
        + positions[:, 1:2] * directions[None, :, 1]
        + positions[:, 2:3] * directions[None, :, 2]
    )
    cosine = jnp.cos(phases)
    sine_part = jnp.sin(phases)
    chosen = jnp.einsum("cmt,td->cmd", pattern, select, precision=HIGHEST_PRECISION)
    inc_real = cosine[None] * chosen[0][:, None, :] - sine_part[None] * chosen[1][:, None, :]
    inc_imag = cosine[None] * chosen[1][:, None, :] + sine_part[None] * chosen[0][:, None, :]
    return (inc_real, inc_imag)


def translate(trans_table, classes, block_values):
    item_count = classes.shape[0]
    mode_count = trans_table.shape[2]
    grouped_classes = classes.reshape(item_count // 8, 8)
    grouped_values = block_values.reshape((item_count // 8, 8) + block_values.shape[1:])

    def one_group(group_items):
        picked, values = group_items
        tables = trans_table[picked]
        data_real = values[:, :mode_count]
        data_imag = values[:, mode_count:]
        part_real = jnp.einsum(
            "kij,kjc->kic", tables[:, 0], data_real, preferred_element_type=jnp.float32
        ) - jnp.einsum("kij,kjc->kic", tables[:, 1], data_imag, preferred_element_type=jnp.float32)
        part_imag = jnp.einsum(
            "kij,kjc->kic", tables[:, 1], data_real, preferred_element_type=jnp.float32
        ) + jnp.einsum("kij,kjc->kic", tables[:, 0], data_imag, preferred_element_type=jnp.float32)
        return jnp.concatenate([part_real, part_imag], 1).astype(jnp.bfloat16)

    return lax.map(one_group, (grouped_classes, grouped_values)).reshape(block_values.shape)


def shards(
    positions,
    wave_vectors,
    pattern,
    dir_index,
    mie,
    trans_table,
    pair_route,
    pair_source,
    pair_target,
    pair_class,
):
    mode_count = pattern.shape[1]
    spheres = positions.shape[0]
    directions = dir_index.shape[0]
    columns = BLOCK * directions
    block_count = spheres // BLOCK
    devices = lax.axis_size("sph")
    pair_count = pair_source.shape[0]
    capacity = max(2, 2 * pair_count // devices)
    slot_count = devices * capacity
    inc_real, inc_imag = incident_field(positions, wave_vectors, pattern, dir_index)
    mie_real = mie[0][:, :, None]
    mie_imag = mie[1][:, :, None]
    scat_real = mie_real * inc_real - mie_imag * inc_imag
    scat_imag = mie_real * inc_imag + mie_imag * inc_real
    coeffs = jnp.concatenate([scat_real, scat_imag], 0).astype(jnp.bfloat16)
    block_data = coeffs.reshape(2 * mode_count, block_count, columns).transpose(1, 0, 2)
    dest_device = pair_route[:, 0]
    by_device = (dest_device[:, None] == jnp.arange(devices, dtype=jnp.int32)[None, :]).astype(
        jnp.int32
    )
    before = jnp.cumsum(by_device, axis=0) - by_device
    rank_in = jnp.sum(before * by_device, axis=1)
    slot_of = dest_device * capacity + rank_in
    slot_match = (jnp.arange(slot_count, dtype=jnp.int32)[:, None] == slot_of[None, :]).astype(
        jnp.int32
    )
    filled = jnp.sum(slot_match, axis=1)
    slot_pair = jnp.sum(slot_match * jnp.arange(pair_count, dtype=jnp.int32)[None, :], axis=1)
    slot_target = jnp.where(filled > 0, pair_target[slot_pair], -1)
    keep_slot = filled.astype(jnp.bfloat16)[:, None, None]
    computed = translate(trans_table, pair_class, block_data[pair_source])
    outgoing = computed[slot_pair] * keep_slot
    outgoing = outgoing.reshape(devices, capacity, 2 * mode_count, columns)
    arrived = lax.all_to_all(outgoing, "sph", split_axis=0, concat_axis=0, tiled=True)
    targets = lax.all_to_all(
        slot_target.reshape(devices, capacity), "sph", split_axis=0, concat_axis=0, tiled=True
    ).reshape(slot_count)
    partial_value = arrived.reshape(slot_count, 2 * mode_count, columns)
    gather_matrix = (jnp.arange(block_count, dtype=jnp.int32)[:, None] == targets[None, :]).astype(
        jnp.bfloat16
    )
    summed = jnp.dot(
        gather_matrix,
        partial_value.reshape(slot_count, 2 * mode_count * columns),
        preferred_element_type=jnp.float32,
    )
    summed = (
        summed.reshape(block_count, 2 * mode_count, columns)
        .transpose(1, 0, 2)
        .reshape(2 * mode_count, spheres, directions)
    )
    total_real = inc_real + summed[:mode_count]
    total_imag = inc_imag + summed[mode_count:]
    out_real = mie_real * total_real - mie_imag * total_imag
    out_imag = mie_real * total_imag + mie_imag * total_real
    scattered = (
        jnp.concatenate([out_real, out_imag], 0)
        .reshape(2 * mode_count, spheres * directions)
        .astype(jnp.bfloat16)
    )
    local_ext = jnp.sum(inc_real * out_real + inc_imag * out_imag, axis=(0, 1))
    extinction = lax.psum(local_ext, "sph")
    return (scattered, extinction)


def solution(mesh):
    placed = (
        P("sph", None),
        P(),
        P(),
        P("groups"),
        P(None, None, "sph"),
        P(),
        P("sph", None),
        P("sph"),
        P("sph"),
        P("sph"),
    )
    return jax.shard_map(
        shards,
        mesh=mesh,
        in_specs=placed,
        out_specs=(P(None, ("groups", "sph")), P("groups")),
        check_vma=False,
    )
```

profile of v0, /device:TPU:0, one launch (start us, length us, event | category | flops | bytes accessed | tf_op | source)
XLA Modules:
  0.0 671.2 jit_solution(2450275542576880069)
XLA Ops:
  3.2 1.6 gather_fusion.1
  5.5 7.4 %all-to-all-start = ((s32[16,1,8]{2,1,0:T(1,128)}), s32[16,1,8]{2,1,0:T(1,128)S(1)}, u32[]{:S(2)}, u32[]{:S(2)}) async-start(s32[16,1,8]{2,1,0:T(1,128)} %bitcast.24), calls=%async_computation | async-start | bytes 16384 | tf_op jit(solution)/shard_map/all_to_all | solution.py:97
  16.3 1.2 convolution_bitcast_fusion
  21.9 4.3 gather_fusion.2
  26.3 134.5 %while.10 = (s32[]{:T(128)}, bf16[8,8,896,64]{2,3,1,0:T(8,128)(2,1)}, s32[8,8]{1,0:T(8,128)S(1)}, bf16[8,2,448,448]{3,2,1,0:T(8,128)(2,1)}, bf16[8,8,896,64]{2,3,1,0:T(8,128)(2,1)}, /*index=5*/s32[]{:T(128)}) while((s32[]{:T(128)}, bf16[8,8,896,64]{2,3,1,0:T(8,128)(2,1)}, s32[8,8]{1,0:T(8,128)S(1)}, bf16[8,2,448,448]{3,2,1,0:T(8,128)(2,1)}, ...), condition=%wide.region_5.6_spmd, body=%wide.region_4.5_spmd.sunk | while | flops 824837120 | bytes 63836904 | solution.py:48
  26.3 7.0 %gather_fusion = bf16[8,2,448,448]{3,2,1,0:T(8,128)(2,1)} fusion(bf16[8,2,448,448]{3,2,1,0:T(8,128)(2,1)} %get-tuple-element.133, s32[1024]{0:T(1024)S(1)} %pad_clamp_fusion.4), kind=kCustom, calls=%fused_computation.clone.1 | custom fusion | bytes 12845088 | tf_op jit(solution)/shard_map/while/body/eval_jaxpr/gather | solution.py:37
  33.3 1.4 dynamic-slice_bitcast_fusion.2
  34.7 3.5 fusion.68
  38.2 1.2 fusion.69
  41.8 1.3 maximum_dynamic-update-slice_fusion.2
  43.1 7.0 %gather_fusion = bf16[8,2,448,448]{3,2,1,0:T(8,128)(2,1)} fusion(bf16[8,2,448,448]{3,2,1,0:T(8,128)(2,1)} %get-tuple-element.133, s32[1024]{0:T(1024)S(1)} %pad_clamp_fusion.4), kind=kCustom, calls=%fused_computation.clone.1 | custom fusion | bytes 12845088 | tf_op jit(solution)/shard_map/while/body/eval_jaxpr/gather | solution.py:37
  50.1 1.4 dynamic-slice_bitcast_fusion.2
  51.5 3.5 fusion.68
  55.0 1.2 fusion.69
  56.2 1.2 fusion.66
  58.6 1.3 maximum_dynamic-update-slice_fusion.2
  59.9 7.0 %gather_fusion = bf16[8,2,448,448]{3,2,1,0:T(8,128)(2,1)} fusion(bf16[8,2,448,448]{3,2,1,0:T(8,128)(2,1)} %get-tuple-element.133, s32[1024]{0:T(1024)S(1)} %pad_clamp_fusion.4), kind=kCustom, calls=%fused_computation.clone.1 | custom fusion | bytes 12845088 | tf_op jit(solution)/shard_map/while/body/eval_jaxpr/gather | solution.py:37
  66.9 1.4 dynamic-slice_bitcast_fusion.2
  68.3 3.5 fusion.68
  71.8 1.2 fusion.69
  73.0 1.2 fusion.66
  75.4 1.3 maximum_dynamic-update-slice_fusion.2
  76.7 7.0 %gather_fusion = bf16[8,2,448,448]{3,2,1,0:T(8,128)(2,1)} fusion(bf16[8,2,448,448]{3,2,1,0:T(8,128)(2,1)} %get-tuple-element.133, s32[1024]{0:T(1024)S(1)} %pad_clamp_fusion.4), kind=kCustom, calls=%fused_computation.clone.1 | custom fusion | bytes 12845088 | tf_op jit(solution)/shard_map/while/body/eval_jaxpr/gather | solution.py:37
  83.7 1.4 dynamic-slice_bitcast_fusion.2
  85.1 3.5 fusion.68
  88.6 1.2 fusion.69
  89.8 1.2 fusion.66
  92.2 1.3 maximum_dynamic-update-slice_fusion.2
  93.5 7.0 %gather_fusion = bf16[8,2,448,448]{3,2,1,0:T(8,128)(2,1)} fusion(bf16[8,2,448,448]{3,2,1,0:T(8,128)(2,1)} %get-tuple-element.133, s32[1024]{0:T(1024)S(1)} %pad_clamp_fusion.4), kind=kCustom, calls=%fused_computation.clone.1 | custom fusion | bytes 12845088 | tf_op jit(solution)/shard_map/while/body/eval_jaxpr/gather | solution.py:37
  100.5 1.4 dynamic-slice_bitcast_fusion.2
  101.9 3.5 fusion.68
  105.4 1.2 fusion.69
  106.6 1.2 fusion.66
  109.0 1.3 maximum_dynamic-update-slice_fusion.2
  110.3 7.0 %gather_fusion = bf16[8,2,448,448]{3,2,1,0:T(8,128)(2,1)} fusion(bf16[8,2,448,448]{3,2,1,0:T(8,128)(2,1)} %get-tuple-element.133, s32[1024]{0:T(1024)S(1)} %pad_clamp_fusion.4), kind=kCustom, calls=%fused_computation.clone.1 | custom fusion | bytes 12845088 | tf_op jit(solution)/shard_map/while/body/eval_jaxpr/gather | solution.py:37
  117.3 1.4 dynamic-slice_bitcast_fusion.2
  118.7 3.5 fusion.68
  122.2 1.2 fusion.69
  123.4 1.2 fusion.66
  125.8 1.3 maximum_dynamic-update-slice_fusion.2
  127.1 7.0 %gather_fusion = bf16[8,2,448,448]{3,2,1,0:T(8,128)(2,1)} fusion(bf16[8,2,448,448]{3,2,1,0:T(8,128)(2,1)} %get-tuple-element.133, s32[1024]{0:T(1024)S(1)} %pad_clamp_fusion.4), kind=kCustom, calls=%fused_computation.clone.1 | custom fusion | bytes 12845088 | tf_op jit(solution)/shard_map/while/body/eval_jaxpr/gather | solution.py:37
  134.1 1.4 dynamic-slice_bitcast_fusion.2
  135.5 3.4 fusion.68
  139.0 1.2 fusion.69
  140.2 1.2 fusion.66
  142.6 1.3 maximum_dynamic-update-slice_fusion.2
  144.0 7.0 %gather_fusion = bf16[8,2,448,448]{3,2,1,0:T(8,128)(2,1)} fusion(bf16[8,2,448,448]{3,2,1,0:T(8,128)(2,1)} %get-tuple-element.133, s32[1024]{0:T(1024)S(1)} %pad_clamp_fusion.4), kind=kCustom, calls=%fused_computation.clone.1 | custom fusion | bytes 12845088 | tf_op jit(solution)/shard_map/while/body/eval_jaxpr/gather | solution.py:37
  151.0 1.4 dynamic-slice_bitcast_fusion.2
  152.4 3.5 fusion.68
  155.9 1.2 fusion.69
  157.1 1.2 fusion.66
  159.5 1.3 maximum_dynamic-update-slice_fusion.2
  160.7 12.3 %gather_fusion.3 = bf16[128,896,64]{1,2,0:T(8,128)(2,1)} fusion(bf16[64,896,64]{1,2,0:T(8,128)(2,1)} %bitcast.33, s32[1024]{0:T(1024)S(1)} %pad_clamp_fusion.2), kind=kCustom, calls=%fused_computation.3 | custom fusion | bytes 29360640 | tf_op jit(solution)/shard_map/gather | solution.py:94
  173.1 13.5 %broadcast_multiply_fusion = bf16[16,8,896,64]{2,3,1,0:T(8,128)(2,1)} fusion(bf16[16,8,896,64]{2,3,1,0:T(8,128)(2,1)} %bitcast.236, bf16[16,8]{1,0:T(8,128)(2,1)S(1)} %convert_element_type.32), kind=kLoop, calls=%fused_computation.29 | loop fusion | flops 7340032 | bytes 29360384 | tf_op jit(solution)/shard_map/mul | solution.py:94
  186.6 6.0 all-to-all-start.1
  194.7 258.1 %all-to-all-done.1 = bf16[16,8,896,64]{2,3,1,0:T(8,128)(2,1)} async-done(((bf16[16,8,896,64]{2,3,1,0:T(8,128)(2,1)}), bf16[16,8,896,64]{2,3,1,0:T(8,128)(2,1)}, u32[]{:S(2)}, u32[]{:S(2)}) %all-to-all-start.1) | async-done | bytes 14680096 | tf_op jit(solution)/shard_map/all_to_all | solution.py:96
  452.8 26.5 %copy.80 = bf16[16,8,896,64]{3,2,1,0:T(8,128)(2,1)} copy(bf16[16,8,896,64]{2,3,1,0:T(8,128)(2,1)} %all-to-all-done.1) | data formatting | bytes 29360128 | tf_op jit(solution)/shard_map/all_to_all | solution.py:96
  479.3 28.1 %reshape_reshape.3 = bf16[128,57344]{1,0:T(8,128)(2,1)} reshape(bf16[16,8,896,64]{3,2,1,0:T(8,128)(2,1)} %copy.80) | data formatting | bytes 29360128 | tf_op jit(solution)/shard_map/reshape;reshape | solution.py:106
  507.4 20.2 %copy.81 = bf16[57344,128]{1,0:T(8,128)(2,1)} copy(bf16[57344,128]{0,1:T(8,128)(2,1)} %bitcast.238) | data formatting | bytes 29360128 | tf_op jit(solution)/shard_map/dot_general | solution.py:104
  527.6 35.5 %fusion.34 = f32[896,16,64]{0,1,2:T(8,128)} fusion(bf16[896,64,128]{2,1,0:T(8,128)(2,1)} %bitcast.237, s32[128]{0:T(128)S(1)} %eq.64), kind=kOutput, calls=%fused_computation.61 | convolution fusion | flops 234883072 | bytes 18350592 | tf_op jit(solution)/shard_map/dot_general | solution.py:104
  563.1 9.9 %add_reduce_fusion = (f32[16,64]{0,1:T(8,128)S(1)}, f32[448,16,64]{0,1,2:T(8,128)S(1)}, f32[448,16,64]{0,1,2:T(8,128)S(1)}) fusion(f32[448,16,64]{0,2,1:T(8,128)S(1)} %bitcast.241, f32[448,16,64]{0,2,1:T(8,128)} %bitcast.247, f32[448,16,64]{0,2,1:T(8,128)S(1)} %bitcast.243, f32[448,16,64]{0,2,1:T(8,128)S(1)} %bitcast.245, f32[16,64]{0,1:T(8,128)S(1)} %copy.87, ...), kind=kLoop, calls=%fused_computation.60 | loop fusion | flops 8256512 | bytes 14692352 | tf_op jit(solution)/shard_map/reduce_sum | solution.py:123
  575.6 1.7 fusion.19
  577.8 2.4 copy.96
  580.4 90.4 %psum.7 = f32[32]{0:T(128)} all-reduce(f32[32]{0:T(128)S(1)} %reduce_sum.51), channel_id=1, replica_groups=mesh['groups'=2,'sph'=16] {'sph'}, use_global_device_ids=true, to_apply=%region_8.9 | all-reduce | flops 32 | bytes 256 | tf_op jit(solution)/shard_map/psum | solution.py:124
  (152 shorter events, 26.9 us)
Async XLA Ops:
  0.6 15.6 %copy-start = (f32[2,448,256]{2,1,0:T(8,128)S(1)}, f32[2,448,256]{2,1,0:T(8,128)}, u32[]{:S(2)}) copy-start(f32[2,448,256]{2,1,0:T(8,128)} %param.14) | copy-start | bytes 2752516
  0.6 16.9 %copy-start.20 = (s32[64]{0:T(128)S(1)}, s32[64]{0:T(128)}, u32[]{:S(2)}) copy-start(s32[64]{0:T(128)} %param.19) | copy-start | bytes 772
  0.7 16.9 %copy-start.19 = (s32[64]{0:T(128)S(1)}, s32[64]{0:T(128)}, u32[]{:S(2)}) copy-start(s32[64]{0:T(128)} %param.21) | copy-start | bytes 772
  0.7 17.0 %copy-start.18 = (f32[2,448,32]{1,2,0:T(8,128)S(1)}, f32[2,448,32]{1,2,0:T(8,128)}, u32[]{:S(2)}) copy-start(f32[2,448,32]{1,2,0:T(8,128)} %param.16) | copy-start | bytes 344068
  5.5 181.1 %all-to-all-start = ((s32[16,1,8]{2,1,0:T(1,128)}), s32[16,1,8]{2,1,0:T(1,128)S(1)}, u32[]{:S(2)}, u32[]{:S(2)}) async-start(s32[16,1,8]{2,1,0:T(1,128)} %bitcast.24), calls=%async_computation | async-start | bytes 16384 | tf_op jit(solution)/shard_map/all_to_all | solution.py:97
  17.7 0.6 copy-start.12
  17.7 0.6 copy-start.14
  17.7 0.6 copy-start.10
  17.7 0.9 copy-start.16
  18.0 1.3 copy-start.3
  18.3 1.7 copy-start.5
  18.6 2.5 copy-start.7
  18.9 2.5 copy-start.9
  33.3 4.9 copy-start.2
  50.1 4.9 copy-start.2
  66.9 4.9 copy-start.2
  83.7 4.9 copy-start.2
  100.5 4.9 copy-start.2
  117.3 4.9 copy-start.2
  134.1 4.9 copy-start.2
  151.0 4.9 copy-start.2
  186.6 266.2 %all-to-all-start.1 = ((bf16[16,8,896,64]{2,3,1,0:T(8,128)(2,1)}), bf16[16,8,896,64]{2,3,1,0:T(8,128)(2,1)}, u32[]{:S(2)}, u32[]{:S(2)}) async-start(bf16[16,8,896,64]{2,3,1,0:T(8,128)(2,1)} %broadcast_multiply_fusion), calls=%async_computation.1 | async-start | bytes 29360128 | tf_op jit(solution)/shard_map/all_to_all | solution.py:96
  527.6 35.5 %copy-start.4 = (f32[448,32,32]{0,2,1:T(8,128)S(1)}, f32[448,32,32]{0,2,1:T(8,128)}, u32[]{:S(2)}) copy-start(f32[448,32,32]{0,2,1:T(8,128)} %copy-done.3) | copy-start | bytes 5505028
  527.6 35.5 %copy-start.6 = (f32[448,32,32]{0,2,1:T(8,128)S(1)}, f32[448,32,32]{0,2,1:T(8,128)}, u32[]{:S(2)}) copy-start(f32[448,32,32]{0,2,1:T(8,128)} %copy-done.5) | copy-start | bytes 5505028
  527.6 35.5 %copy-start.8 = (f32[448,32,32]{0,2,1:T(8,128)S(1)}, f32[448,32,32]{0,2,1:T(8,128)}, u32[]{:S(2)}) copy-start(f32[448,32,32]{0,2,1:T(8,128)} %copy-done.7) | copy-start | bytes 5505028
  574.3 1.3 copy-start.11
  574.3 1.3 copy-start.13
  574.3 1.3 copy-start.15
  574.3 1.3 copy-start.17
  577.2 93.6 %copy-start.1 = (f32[2,448,256]{2,1,0:T(8,128)S(1)}, f32[2,448,256]{2,1,0:T(8,128)}, u32[]{:S(2)}) copy-start(f32[2,448,256]{2,1,0:T(8,128)} %param.14) | copy-start | bytes 2752516
where the time goes:
time: 683 us; the launch traced here: 671 us
  waiting for transfers between devices  258 us (38%)
  local copies, waits for them, and re-layouts  172 us (25%)
  matrix products  94.1 us (14%)
  blocking collectives  90.4 us (13%)
  other arithmetic  41 us (6%)
  starting transfers between devices  13.5 us (2%)
    all_to_all x1, waiting for transfers between devices, shards(): lax.all_to_all(outgoing, 'sph', split_axis=0, concat_axis=0, tiled=True)  258 us
    psum x1, blocking collectives, shards(): extinction = lax.psum(local_ext, 'sph')  90.4 us
    gather x8, local copies, waits for them, and re-layouts, one_group(): tables = trans_table[picked]  56.2 us
    dot_general x1, matrix products, shards(): jnp.dot(gather_matrix, partial_value.reshape(slot_count, 2 * mode_count *...  35.5 us
    another operation x1, local copies, waits for them, and re-layouts, shards(): partial_value.reshape(slot_count, 2 * mode_count * columns)  28.1 us
    dot_general x8, matrix products, one_group(): jnp.einsum('kij,kjc->kic', tables[:, 0], data_real, preferred_element_typ...  27.6 us
    all_to_all x1, local copies, waits for them, and re-layouts, shards(): lax.all_to_all(outgoing, 'sph', split_axis=0, concat_axis=0, tiled=True)  26.5 us
    dot_general x1, local copies, waits for them, and re-layouts, shards(): jnp.dot(gather_matrix, partial_value.reshape(slot_count, 2 * mode_count *...  20.2 us
  transfers between devices with their start and end apart: 2, of which 1 were waited for; matrix products, arithmetic and copies ran while one was open for 26% of the time, Pallas kernels for 0%

commit v1 on v0

--- a/solution.py
+++ b/solution.py
@@ -5,6 +5,21 @@
 
 BLOCK = 2
 HIGHEST_PRECISION = lax.Precision.HIGHEST
+
+
+def manage_notes_in(x_part, join_dim, local):
+    u1 = x_part.shape
+    return jnp.moveaxis(
+        x_part.reshape(*u1[:join_dim], local, u1[join_dim] // local, *u1[join_dim + 1 :]),
+        join_dim,
+        0,
+    )
+
+
+def detail_stages_all(page, which_dim):
+    a_now = list(page.shape[1:])
+    a_now[which_dim] *= page.shape[0]
+    return jnp.moveaxis(page, 0, which_dim).reshape(a_now)
 
 
 def incident_field(positions, wave_vectors, pattern, dir_index):
@@ -93,7 +108,18 @@
     computed = translate(trans_table, pair_class, block_data[pair_source])
     outgoing = computed[slot_pair] * keep_slot
     outgoing = outgoing.reshape(devices, capacity, 2 * mode_count, columns)
-    arrived = lax.all_to_all(outgoing, "sph", split_axis=0, concat_axis=0, tiled=True)
+    upper = lax.psum(1, "sph")
+    y_new, arr_now = (upper, lax.axis_index("sph"))
+    mixed_arr = manage_notes_in(outgoing, 0, y_new)
+    sides = [mixed_arr[arr_now]]
+    for kk in range(1, y_new):
+        passed = mixed_arr[arr_now ^ kk]
+        r_now = lax.ppermute(
+            passed, axis_name="sph", perm=[(dev_j, dev_j ^ kk) for dev_j in range(y_new)]
+        )
+        sides.append(r_now)
+    mixed_arr = jnp.stack(sides, axis=0)[arr_now ^ jnp.arange(y_new)]
+    arrived = detail_stages_all(mixed_arr, 0)
     targets = lax.all_to_all(
         slot_target.reshape(devices, capacity), "sph", split_axis=0, concat_axis=0, tiled=True
     ).reshape(slot_count)

time: 683 us -> 753 us (1.10)
  local copies, waits for them, and re-layouts: 172 us -> 216 us
  starting transfers between devices: 13.5 us -> 25.4 us
  matrix products: 94.1 us -> 103 us
  blocking collectives: 90.4 us -> 98.9 us
    all_to_all x1 -> x0, waiting for transfers between devices: 258 us -> none  [shards(): lax.all_to_all(outgoing, 'sph', split_axis=0, concat_axis=0, tiled=True)]
    ppermute x0 -> x15, waiting for transfers between devices: none -> 220 us  [shards(): lax.ppermute(passed, axis_name='sph', perm=[(dev_j, dev_j ^ kk) for dev_j...]
    gather x0 -> x2, local copies, waits for them, and re-layouts: none -> 39.4 us  [shards(): mixed_arr = jnp.stack(sides, axis=0)[arr_now ^ jnp.arange(y_new)]]
    all_to_all x1, waiting for transfers between devices: 0.01 us -> 36.2 us  [shards(): lax.all_to_all(slot_target.reshape(devices, capacity), 'sph', split_axis=...]
    all_to_all x1 -> x0, local copies, waits for them, and re-layouts: 26.5 us -> none  [shards(): lax.all_to_all(outgoing, 'sph', split_axis=0, concat_axis=0, tiled=True)]
    ppermute x0 -> x15, starting transfers between devices: none -> 19 us  [shards(): lax.ppermute(passed, axis_name='sph', perm=[(dev_j, dev_j ^ kk) for dev_j...]
    unnamed x41 -> x67, local copies, waits for them, and re-layouts: 3.94 us -> 20.8 us
    squeeze x0 -> x1, local copies, waits for them, and re-layouts: none -> 10.8 us  [shards(): passed = mixed_arr[arr_now ^ kk]]
  transfers between devices with their start and end apart: 2 -> 16, of which waited for: 1 -> 6; matrix products, arithmetic and copies ran while one was open for 26% -> 3% of each run, Pallas kernels for 0% -> 0%
where the time goes in v1:
time: 753 us; the launch traced here: 743 us
  waiting for transfers between devices  256 us (34%)
  local copies, waits for them, and re-layouts  216 us (29%)
  matrix products  103 us (14%)
  blocking collectives  98.9 us (13%)
  other arithmetic  41.6 us (6%)
  starting transfers between devices  25.4 us (3%)
    ppermute x15, waiting for transfers between devices, shards(): lax.ppermute(passed, axis_name='sph', perm=[(dev_j, dev_j ^ kk) for dev_j...  220 us
    psum x1, blocking collectives, shards(): extinction = lax.psum(local_ext, 'sph')  98.9 us
    gather x8, local copies, waits for them, and re-layouts, one_group(): tables = trans_table[picked]  57 us
    dot_general x1, matrix products, shards(): jnp.dot(gather_matrix, partial_value.reshape(slot_count, 2 * mode_count *...  44 us
    gather x2, local copies, waits for them, and re-layouts, shards(): mixed_arr = jnp.stack(sides, axis=0)[arr_now ^ jnp.arange(y_new)]  39.4 us
    all_to_all x1, waiting for transfers between devices, shards(): lax.all_to_all(slot_target.reshape(devices, capacity), 'sph', split_axis=...  36.2 us
    another operation x1, local copies, waits for them, and re-layouts, shards(): partial_value.reshape(slot_count, 2 * mode_count * columns)  28.1 us
    dot_general x8, matrix products, one_group(): jnp.einsum('kij,kjc->kic', tables[:, 0], data_real, preferred_element_typ...  27.6 us
  transfers between devices with their start and end apart: 16, of which 6 were waited for; matrix products, arithmetic and copies ran while one was open for 3% of the time, Pallas kernels for 0%

profile of v1, /device:TPU:0, one launch (start us, length us, event | category | flops | bytes accessed | tf_op | source)
XLA Modules:
  0.0 742.5 jit_solution(17099365467838386566)
XLA Ops:
  14.3 4.3 gather_fusion.2
  18.6 135.3 %while.10 = (s32[]{:T(128)}, bf16[8,8,896,64]{2,3,1,0:T(8,128)(2,1)}, s32[8,8]{1,0:T(8,128)S(1)}, bf16[8,2,448,448]{3,2,1,0:T(8,128)(2,1)}, bf16[8,8,896,64]{2,3,1,0:T(8,128)(2,1)}, /*index=5*/s32[]{:T(128)}) while((s32[]{:T(128)}, bf16[8,8,896,64]{2,3,1,0:T(8,128)(2,1)}, s32[8,8]{1,0:T(8,128)S(1)}, bf16[8,2,448,448]{3,2,1,0:T(8,128)(2,1)}, ...), condition=%wide.region_5.6_spmd, body=%wide.region_4.5_spmd.sunk | while | flops 824837120 | bytes 63836904 | solution.py:63
  18.6 7.1 gather_fusion
  25.8 1.4 dynamic-slice_bitcast_fusion.17
  27.2 3.5 fusion.69
  34.3 1.3 maximum_dynamic-update-slice_fusion.2
  35.5 7.1 gather_fusion
  42.7 1.4 dynamic-slice_bitcast_fusion.17
  44.1 3.4 fusion.69
  51.2 1.3 maximum_dynamic-update-slice_fusion.2
  52.4 7.1 gather_fusion
  59.6 1.4 dynamic-slice_bitcast_fusion.17
  61.0 3.5 fusion.69
  68.1 1.3 maximum_dynamic-update-slice_fusion.2
  69.4 7.1 gather_fusion
  76.5 1.4 dynamic-slice_bitcast_fusion.17
  77.9 3.5 fusion.69
  85.0 1.3 maximum_dynamic-update-slice_fusion.2
  86.3 7.1 gather_fusion
  93.4 1.4 dynamic-slice_bitcast_fusion.17
  94.8 3.5 fusion.69
  101.9 1.3 maximum_dynamic-update-slice_fusion.2
  103.2 7.1 gather_fusion
  110.4 1.4 dynamic-slice_bitcast_fusion.17
  111.8 3.5 fusion.69
  118.8 1.3 maximum_dynamic-update-slice_fusion.2
  120.1 7.1 gather_fusion
  127.3 1.4 dynamic-slice_bitcast_fusion.17
  128.7 3.5 fusion.69
  132.1 1.2 fusion.70
  135.8 1.3 maximum_dynamic-update-slice_fusion.2
  137.0 7.1 gather_fusion
  144.2 1.4 dynamic-slice_bitcast_fusion.17
  145.6 3.5 fusion.69
  152.7 1.3 maximum_dynamic-update-slice_fusion.2
  154.0 12.3 %gather_fusion.3 = bf16[128,896,64]{1,2,0:T(8,128)(2,1)} fusion(bf16[64,896,64]{1,2,0:T(8,128)(2,1)} %bitcast.33, s32[1024]{0:T(1024)S(1)} %get-tuple-element.104), kind=kCustom, calls=%fused_computation.3 | custom fusion | bytes 29360640 | tf_op jit(solution)/shard_map/gather | solution.py:109
  167.6 13.5 %broadcast_multiply_fusion = bf16[16,1,8,896,64]{3,4,2,0,1:T(8,128)(2,1)} fusion(bf16[16,1,8,896,64]{3,4,2,0,1:T(8,128)(2,1)} %bitcast.299, bf16[16,8]{1,0:T(8,128)(2,1)S(1)} %convert_element_type.32), kind=kLoop, calls=%fused_computation.30 | loop fusion | flops 7340032 | bytes 29360384 | tf_op jit(solution)/shard_map/mul | solution.py:109
  181.1 10.8 %dynamic-slice_bitcast_fusion.1 = (bf16[1,8,896,64]{2,3,1,0:T(8,128)(2,1)}, bf16[1,8,896,64]{2,3,1,0:T(8,128)(2,1)}, bf16[1,8,896,64]{2,3,1,0:T(8,128)(2,1)}, bf...) fusion(bf16[16,1,8,896,64]{3,4,2,0,1:T(8,128)(2,1)} %broadcast_, ...), kind=kLoop, calls=%fused_computation.81 | loop fusion | bytes 29360192 | tf_op jit(solution)/shard_map/squeeze | solution.py:116
  192.5 2.6 collective-permute-start.1
  195.1 1.8 collective-permute-start.3
  197.6 6.4 all-to-all-start
  204.8 36.2 %all-to-all-done = s32[16,1,8]{2,1,0:T(1,128)S(1)} async-done(((s32[16,1,8]{2,1,0:T(1,128)}), s32[16,1,8]{2,1,0:T(1,128)S(1)}, u32[]{:S(2)}, u32[]{:S(2)}) %all-to-all-start) | async-done | bytes 544 | tf_op jit(solution)/shard_map/all_to_all | solution.py:123
  242.8 2.3 bitcast_dynamic-update-slice_fusion.14
  245.1 1.5 collective-permute-start.6
  246.7 2.2 bitcast_dynamic-update-slice_fusion.13
  250.5 2.7 collective-permute-start.8
  255.9 42.6 %collective-permute-done.5 = bf16[1,8,896,64]{2,3,1,0:T(8,128)(2,1)S(1)} collective-permute-done((bf16[1,8,896,64]{2,3,1,0:T(8,128)(2,1)}, bf16[1,8,896,64]{2,3,1,0:T(8,128)(2,1)S(1)}, u32[]{:S(2)}, u32[]{:S(2)}) %collective-permute-start.5) | collective-permute-done | bytes 917536 | tf_op jit(solution)/shard_map/ppermute | solution.py:117
  299.5 16.3 %collective-permute-done.6 = bf16[1,8,896,64]{2,3,1,0:T(8,128)(2,1)S(1)} collective-permute-done((bf16[1,8,896,64]{2,3,1,0:T(8,128)(2,1)}, bf16[1,8,896,64]{2,3,1,0:T(8,128)(2,1)S(1)}, u32[]{:S(2)}, u32[]{:S(2)}) %collective-permute-start.6) | collective-permute-done | bytes 917536 | tf_op jit(solution)/shard_map/ppermute | solution.py:117
  315.8 2.4 collective-permute-start.11
  319.2 2.1 collective-permute-start.12
  322.3 88.4 %collective-permute-done.8 = bf16[1,8,896,64]{2,3,1,0:T(8,128)(2,1)S(1)} collective-permute-done((bf16[1,8,896,64]{2,3,1,0:T(8,128)(2,1)S(1)}, bf16[1,8,896,64]{2,3,1,0:T(8,128)(2,1)S(1)}, u32[]{:S(2)}, u32[]{:S(2)}) %collective-permute-start.8) | collective-permute-done | bytes 917536 | tf_op jit(solution)/shard_map/ppermute | solution.py:117
  410.8 1.3 collective-permute-start.13
  413.2 36.9 %collective-permute-done.9 = bf16[1,8,896,64]{2,3,1,0:T(8,128)(2,1)S(1)} collective-permute-done((bf16[1,8,896,64]{2,3,1,0:T(8,128)(2,1)S(1)}, bf16[1,8,896,64]{2,3,1,0:T(8,128)(2,1)S(1)}, u32[]{:S(2)}, u32[]{:S(2)}) %collective-permute-start.9) | collective-permute-done | bytes 917536 | tf_op jit(solution)/shard_map/ppermute | solution.py:117
  450.1 2.2 collective-permute-start.14
  453.3 36.0 %collective-permute-done.10 = bf16[1,8,896,64]{2,3,1,0:T(8,128)(2,1)S(1)} collective-permute-done((bf16[1,8,896,64]{2,3,1,0:T(8,128)(2,1)S(1)}, bf16[1,8,896,64]{2,3,1,0:T(8,128)(2,1)S(1)}, u32[]{:S(2)}, u32[]{:S(2)}) %collective-permute-start.10) | collective-permute-done | bytes 917536 | tf_op jit(solution)/shard_map/ppermute | solution.py:117
  494.5 12.8 %gather_fusion.4 = bf16[16,8,896,64]{2,3,1,0:T(8,128)(2,1)} fusion(bf16[16,8,896,64]{2,3,1,0:T(8,128)(2,1)} %bitcast.300, s32[1024]{0:T(1024)S(1)} %pad_clamp_fusion.1), kind=kCustom, calls=%fused_computation.4 | custom fusion | bytes 29360192 | tf_op jit(solution)/shard_map/gather | solution.py:121
  507.2 26.6 %copy.97 = bf16[16,8,896,64]{3,2,1,0:T(8,128)(2,1)} copy(bf16[16,8,896,64]{2,3,1,0:T(8,128)(2,1)} %gather_fusion.4) | data formatting | bytes 29360128 | tf_op jit(solution)/shard_map/gather | solution.py:121
  533.8 28.1 %reshape_reshape_reshape.3 = bf16[128,57344]{1,0:T(8,128)(2,1)} reshape(bf16[16,8,896,64]{3,2,1,0:T(8,128)(2,1)} %copy.97) | data formatting | bytes 29360128 | tf_op jit(solution)/shard_map/reshape;reshape;reshape | solution.py:132
  562.0 19.9 %copy.98 = bf16[57344,128]{1,0:T(8,128)(2,1)} copy(bf16[57344,128]{0,1:T(8,128)(2,1)} %bitcast.302) | data formatting | bytes 29360128 | tf_op jit(solution)/shard_map/dot_general | solution.py:130
  581.9 44.0 %fusion.34 = f32[896,16,64]{0,1,2:T(8,128)} fusion(bf16[896,64,128]{2,1,0:T(8,128)(2,1)} %bitcast.301, s32[128]{0:T(128)S(1)} %eq.64), kind=kOutput, calls=%fused_computation.62 | convolution fusion | flops 234883072 | bytes 18350592 | tf_op jit(solution)/shard_map/dot_general | solution.py:130
  625.9 9.9 %add_reduce_fusion = (f32[16,64]{0,1:T(8,128)S(1)}, f32[448,16,64]{0,1,2:T(8,128)S(1)}, f32[448,16,64]{0,1,2:T(8,128)S(1)}) fusion(f32[448,16,64]{0,2,1:T(8,128)S(1)} %bitcast.305, f32[448,16,64]{0,2,1:T(8,128)} %bitcast.311, f32[448,16,64]{0,2,1:T(8,128)S(1)} %bitcast.307, f32[448,16,64]{0,2,1:T(8,128)S(1)} %bitcast.309, f32[16,64]{0,1:T(8,128)S(1)} %copy.104, ...), kind=kLoop, calls=%fused_computation.61 | loop fusion | flops 8256512 | bytes 14692352 | tf_op jit(solution)/shard_map/reduce_sum | solution.py:149
  638.4 1.7 fusion.19
  640.7 2.4 copy.113
  643.2 98.9 %psum.7 = f32[32]{0:T(128)} all-reduce(f32[32]{0:T(128)S(1)} %reduce_sum.51), channel_id=1, replica_groups=mesh['groups'=2,'sph'=16] {'sph'}, use_global_device_ids=true, to_apply=%region_8.9 | all-reduce | flops 32 | bytes 256 | tf_op jit(solution)/shard_map/psum | solution.py:150
  (210 shorter events, 64.4 us)
Async XLA Ops:
  0.6 3.4 copy-start
  10.0 1.1 copy-start.19
  10.0 1.1 copy-start.21
  10.0 1.1 copy-start.23
  10.0 1.1 copy-start.25
  10.3 1.9 copy-start.4
  10.6 1.7 copy-start.6
  10.9 2.0 copy-start.8
  11.2 2.5 copy-start.10
  25.8 4.9 copy-start.3
  42.7 4.9 copy-start.3
  59.6 4.9 copy-start.3
  76.5 4.9 copy-start.3
  93.4 4.9 copy-start.3
  110.4 4.9 copy-start.3
  127.3 4.9 copy-start.3
  144.2 4.9 copy-start.3
  154.0 12.3 %copy-start.2 = (s32[64]{0:T(128)S(1)}, s32[64]{0:T(128)}, u32[]{:S(2)}) copy-start(s32[64]{0:T(128)} %param.20) | copy-start | bytes 772
  191.9 50.3 %collective-permute-start = (bf16[1,8,896,64]{2,3,1,0:T(8,128)(2,1)}, bf16[1,8,896,64]{2,3,1,0:T(8,128)(2,1)}, u32[]{:S(2)}, u32[]{:S(2)}) collective-permute-start(bf16[1,8,896,64]{2,3,1,0:T(8,128)(2,1)} %get-tuple-element.80), channel_id=1, source_target_pairs={{0,1},{1,0},{2,3},{3,2},{4,5},{5,4},{6,7},{7,6},{8,9},{9,8},{10,11... | collective-permute-start | bytes 2752520 | tf_op jit(solution)/shard_map/ppermute | solution.py:117
  192.5 52.7 %collective-permute-start.1 = (bf16[1,8,896,64]{2,3,1,0:T(8,128)(2,1)}, bf16[1,8,896,64]{2,3,1,0:T(8,128)(2,1)}, u32[]{:S(2)}, u32[]{:S(2)}) collective-permute-start(bf16[1,8,896,64]{2,3,1,0:T(8,128)(2,1)} %get-tuple-element.79), channel_id=1, source_target_pairs={{0,2},{1,3},{2,0},{3,1},{4,6},{5,7},{6,4},{7,5},{8,10},{9,11},{10,... | collective-permute-start | bytes 2752520 | tf_op jit(solution)/shard_map/ppermute | solution.py:117
  195.1 53.8 %collective-permute-start.2 = (bf16[1,8,896,64]{2,3,1,0:T(8,128)(2,1)}, bf16[1,8,896,64]{2,3,1,0:T(8,128)(2,1)S(1)}, u32[]{:S(2)}, u32[]{:S(2)}) collective-permute-start(bf16[1,8,896,64]{2,3,1,0:T(8,128)(2,1)} %get-tuple-element.78), channel_id=1, source_target_pairs={{0,3},{1,2},{2,1},{3,0},{4,7},{5,6},{6,5},{7,4},{8,11},{9,10},{10,... | collective-permute-start | bytes 2752520 | tf_op jit(solution)/shard_map/ppermute | solution.py:117
  195.1 55.4 %collective-permute-start.3 = (bf16[1,8,896,64]{2,3,1,0:T(8,128)(2,1)}, bf16[1,8,896,64]{2,3,1,0:T(8,128)(2,1)S(1)}, u32[]{:S(2)}, u32[]{:S(2)}) collective-permute-start(bf16[1,8,896,64]{2,3,1,0:T(8,128)(2,1)} %get-tuple-element.77), channel_id=1, source_target_pairs={{0,4},{1,5},{2,6},{3,7},{4,0},{5,1},{6,2},{7,3},{8,12},{9,13},{10,... | collective-permute-start | bytes 2752520 | tf_op jit(solution)/shard_map/ppermute | solution.py:117
  196.9 57.4 %collective-permute-start.4 = (bf16[1,8,896,64]{2,3,1,0:T(8,128)(2,1)}, bf16[1,8,896,64]{2,3,1,0:T(8,128)(2,1)S(1)}, u32[]{:S(2)}, u32[]{:S(2)}) collective-permute-start(bf16[1,8,896,64]{2,3,1,0:T(8,128)(2,1)} %get-tuple-element.76), channel_id=1, source_target_pairs={{0,5},{1,4},{2,7},{3,6},{4,1},{5,0},{6,3},{7,2},{8,13},{9,12},{10,... | collective-permute-start | bytes 2752520 | tf_op jit(solution)/shard_map/ppermute | solution.py:117
  197.6 43.4 %all-to-all-start = ((s32[16,1,8]{2,1,0:T(1,128)}), s32[16,1,8]{2,1,0:T(1,128)S(1)}, u32[]{:S(2)}, u32[]{:S(2)}) async-start(s32[16,1,8]{2,1,0:T(1,128)} %bitcast.24), calls=%async_computation | async-start | bytes 16384 | tf_op jit(solution)/shard_map/all_to_all | solution.py:123
  242.2 6.6 copy-start.18
  242.2 8.3 %copy-start.17 = (bf16[1,8,896,64]{2,3,1,0:T(8,128)(2,1)S(1)}, bf16[1,8,896,64]{2,3,1,0:T(8,128)(2,1)}, u32[]{:S(2)}) copy-start(bf16[1,8,896,64]{2,3,1,0:T(8,128)(2,1)} %get-tuple-element.72) | copy-start | bytes 2752516
  242.2 56.2 %collective-permute-start.5 = (bf16[1,8,896,64]{2,3,1,0:T(8,128)(2,1)}, bf16[1,8,896,64]{2,3,1,0:T(8,128)(2,1)S(1)}, u32[]{:S(2)}, u32[]{:S(2)}) collective-permute-start(bf16[1,8,896,64]{2,3,1,0:T(8,128)(2,1)} %get-tuple-element.75), channel_id=1, source_target_pairs={{0,6},{1,7},{2,4},{3,5},{4,2},{5,3},{6,0},{7,1},{8,14},{9,15},{10,... | collective-permute-start | bytes 2752520 | tf_op jit(solution)/shard_map/ppermute | solution.py:117
  242.8 11.5 %copy-start.16 = (bf16[1,8,896,64]{2,3,1,0:T(8,128)(2,1)S(1)}, bf16[1,8,896,64]{2,3,1,0:T(8,128)(2,1)}, u32[]{:S(2)}) copy-start(bf16[1,8,896,64]{2,3,1,0:T(8,128)(2,1)} %get-tuple-element.71) | copy-start | bytes 2752516
  245.1 53.3 %copy-start.15 = (bf16[1,8,896,64]{2,3,1,0:T(8,128)(2,1)S(1)}, bf16[1,8,896,64]{2,3,1,0:T(8,128)(2,1)}, u32[]{:S(2)}) copy-start(bf16[1,8,896,64]{2,3,1,0:T(8,128)(2,1)} %get-tuple-element.70) | copy-start | bytes 2752516
  245.1 70.6 %collective-permute-start.6 = (bf16[1,8,896,64]{2,3,1,0:T(8,128)(2,1)}, bf16[1,8,896,64]{2,3,1,0:T(8,128)(2,1)S(1)}, u32[]{:S(2)}, u32[]{:S(2)}) collective-permute-start(bf16[1,8,896,64]{2,3,1,0:T(8,128)(2,1)} %get-tuple-element.74), channel_id=1, source_target_pairs={{0,7},{1,6},{2,5},{3,4},{4,3},{5,2},{6,1},{7,0},{8,15},{9,14},{10,... | collective-permute-start | bytes 2752520 | tf_op jit(solution)/shard_map/ppermute | solution.py:117
  248.9 66.9 %copy-start.14 = (bf16[1,8,896,64]{2,3,1,0:T(8,128)(2,1)S(1)}, bf16[1,8,896,64]{2,3,1,0:T(8,128)(2,1)}, u32[]{:S(2)}) copy-start(bf16[1,8,896,64]{2,3,1,0:T(8,128)(2,1)} %get-tuple-element.69) | copy-start | bytes 2752516
  248.9 70.3 %collective-permute-start.7 = (bf16[1,8,896,64]{2,3,1,0:T(8,128)(2,1)S(1)}, bf16[1,8,896,64]{2,3,1,0:T(8,128)(2,1)S(1)}, u32[]{:S(2)}, u32[]{:S(2)}) collective-permute-start(bf16[1,8,896,64]{2,3,1,0:T(8,128)(2,1)S(1)} %copy-done.18), channel_id=1, source_target_pairs={{0,8},{1,9},{2,10},{3,11},{4,12},{5,13},{6,14},{7,15},{8,0},{9,1},... | collective-permute-start | bytes 2752520 | tf_op jit(solution)/shard_map/ppermute | solution.py:117
  250.5 68.6 %copy-start.13 = (bf16[1,8,896,64]{2,3,1,0:T(8,128)(2,1)S(1)}, bf16[1,8,896,64]{2,3,1,0:T(8,128)(2,1)}, u32[]{:S(2)}) copy-start(bf16[1,8,896,64]{2,3,1,0:T(8,128)(2,1)} %get-tuple-element.68) | copy-start | bytes 2752516
  250.5 160.2 %collective-permute-start.8 = (bf16[1,8,896,64]{2,3,1,0:T(8,128)(2,1)S(1)}, bf16[1,8,896,64]{2,3,1,0:T(8,128)(2,1)S(1)}, u32[]{:S(2)}, u32[]{:S(2)}) collective-permute-start(bf16[1,8,896,64]{2,3,1,0:T(8,128)(2,1)S(1)} %copy-done.17), channel_id=1, source_target_pairs={{0,9},{1,8},{2,11},{3,10},{4,13},{5,12},{6,15},{7,14},{8,1},{9,0},... | collective-permute-start | bytes 2752520 | tf_op jit(solution)/shard_map/ppermute | solution.py:117
  254.3 156.5 %copy-start.12 = (bf16[1,8,896,64]{2,3,1,0:T(8,128)(2,1)S(1)}, bf16[1,8,896,64]{2,3,1,0:T(8,128)(2,1)}, u32[]{:S(2)}) copy-start(bf16[1,8,896,64]{2,3,1,0:T(8,128)(2,1)} %get-tuple-element.67) | copy-start | bytes 2752516
  254.3 195.8 %collective-permute-start.9 = (bf16[1,8,896,64]{2,3,1,0:T(8,128)(2,1)S(1)}, bf16[1,8,896,64]{2,3,1,0:T(8,128)(2,1)S(1)}, u32[]{:S(2)}, u32[]{:S(2)}) collective-permute-start(bf16[1,8,896,64]{2,3,1,0:T(8,128)(2,1)S(1)} %copy-done.16), channel_id=1, source_target_pairs={{0,10},{1,11},{2,8},{3,9},{4,14},{5,15},{6,12},{7,13},{8,2},{9,3},... | collective-permute-start | bytes 2752520 | tf_op jit(solution)/shard_map/ppermute | solution.py:117
  298.5 151.6 %copy-start.11 = (bf16[1,8,896,64]{2,3,1,0:T(8,128)(2,1)S(1)}, bf16[1,8,896,64]{2,3,1,0:T(8,128)(2,1)}, u32[]{:S(2)}) copy-start(bf16[1,8,896,64]{2,3,1,0:T(8,128)(2,1)} %get-tuple-element.66) | copy-start | bytes 2752516
  298.5 190.8 %collective-permute-start.10 = (bf16[1,8,896,64]{2,3,1,0:T(8,128)(2,1)S(1)}, bf16[1,8,896,64]{2,3,1,0:T(8,128)(2,1)S(1)}, u32[]{:S(2)}, u32[]{:S(2)}) collective-permute-start(bf16[1,8,896,64]{2,3,1,0:T(8,128)(2,1)S(1)} %copy-done.15), channel_id=1, source_target_pairs={{0,11},{1,10},{2,9},{3,8},{4,15},{5,14},{6,13},{7,12},{8,3},{9,2},... | collective-permute-start | bytes 2752520 | tf_op jit(solution)/shard_map/ppermute | solution.py:117
  315.8 174.5 %collective-permute-start.11 = (bf16[1,8,896,64]{2,3,1,0:T(8,128)(2,1)S(1)}, bf16[1,8,896,64]{2,3,1,0:T(8,128)(2,1)S(1)}, u32[]{:S(2)}, u32[]{:S(2)}) collective-permute-start(bf16[1,8,896,64]{2,3,1,0:T(8,128)(2,1)S(1)} %copy-done.14), channel_id=1, source_target_pairs={{0,12},{1,13},{2,14},{3,15},{4,8},{5,9},{6,10},{7,11},{8,4},{9,5},... | collective-permute-start | bytes 2752520 | tf_op jit(solution)/shard_map/ppermute | solution.py:117
  319.2 172.2 %collective-permute-start.12 = (bf16[1,8,896,64]{2,3,1,0:T(8,128)(2,1)S(1)}, bf16[1,8,896,64]{2,3,1,0:T(8,128)(2,1)S(1)}, u32[]{:S(2)}, u32[]{:S(2)}) collective-permute-start(bf16[1,8,896,64]{2,3,1,0:T(8,128)(2,1)S(1)} %copy-done.13), channel_id=1, source_target_pairs={{0,13},{1,12},{2,15},{3,14},{4,9},{5,8},{6,11},{7,10},{8,5},{9,4},... | collective-permute-start | bytes 2752520 | tf_op jit(solution)/shard_map/ppermute | solution.py:117
  410.8 81.6 %collective-permute-start.13 = (bf16[1,8,896,64]{2,3,1,0:T(8,128)(2,1)S(1)}, bf16[1,8,896,64]{2,3,1,0:T(8,128)(2,1)S(1)}, u32[]{:S(2)}, u32[]{:S(2)}) collective-permute-start(bf16[1,8,896,64]{2,3,1,0:T(8,128)(2,1)S(1)} %copy-done.12), channel_id=1, source_target_pairs={{0,14},{1,15},{2,12},{3,13},{4,10},{5,11},{6,8},{7,9},{8,6},{9,7},... | collective-permute-start | bytes 2752520 | tf_op jit(solution)/shard_map/ppermute | solution.py:117
  450.1 43.3 %collective-permute-start.14 = (bf16[1,8,896,64]{2,3,1,0:T(8,128)(2,1)S(1)}, bf16[1,8,896,64]{2,3,1,0:T(8,128)(2,1)S(1)}, u32[]{:S(2)}, u32[]{:S(2)}) collective-permute-start(bf16[1,8,896,64]{2,3,1,0:T(8,128)(2,1)S(1)} %copy-done.11), channel_id=1, source_target_pairs={{0,15},{1,14},{2,13},{3,12},{4,11},{5,10},{6,9},{7,8},{8,7},{9,6},... | collective-permute-start | bytes 2752520 | tf_op jit(solution)/shard_map/ppermute | solution.py:117
  581.9 44.0 %copy-start.5 = (f32[448,32,32]{0,2,1:T(8,128)S(1)}, f32[448,32,32]{0,2,1:T(8,128)}, u32[]{:S(2)}) copy-start(f32[448,32,32]{0,2,1:T(8,128)} %copy-done.4) | copy-start | bytes 5505028
  581.9 44.0 %copy-start.7 = (f32[448,32,32]{0,2,1:T(8,128)S(1)}, f32[448,32,32]{0,2,1:T(8,128)}, u32[]{:S(2)}) copy-start(f32[448,32,32]{0,2,1:T(8,128)} %copy-done.6) | copy-start | bytes 5505028
  581.9 44.0 %copy-start.9 = (f32[448,32,32]{0,2,1:T(8,128)S(1)}, f32[448,32,32]{0,2,1:T(8,128)}, u32[]{:S(2)}) copy-start(f32[448,32,32]{0,2,1:T(8,128)} %copy-done.8) | copy-start | bytes 5505028
  635.8 2.5 copy-start.20
  635.9 2.5 copy-start.22
  635.9 2.5 copy-start.24
  635.9 2.5 copy-start.26
  640.0 102.1 %copy-start.1 = (f32[2,448,256]{2,1,0:T(8,128)S(1)}, f32[2,448,256]{2,1,0:T(8,128)}, u32[]{:S(2)}) copy-start(f32[2,448,256]{2,1,0:T(8,128)} %param.14) | copy-start | bytes 2752516
